TPU v7x, 256 devices: a whole 4x4x8 slice. The times are simulated.
256 devices in a mesh: grp: 8 (over z), mem: 32 (over y, x, core).
Axes of the slice: x: 4, y: 4, z: 8, core: 2. Of those that a mesh axis runs over, the one named last changes fastest.
Arguments:
- child_means: float32 [524288, 64], P(('grp', 'mem')), may hold values from -48 to 48
- child_variances: float32 [524288, 64], P(('grp', 'mem')), may hold values from 0.2 to 2
- virtual_counts: int32 [524288], P(('grp', 'mem')), may hold values from 1 to 4
- assignment: int32 [524288, 1], P(('grp', 'mem')), may hold values from 0 to 511
Outputs:
- parent_means: float32 [512, 64], P('mem')
- parent_variances: float32 [512, 64], P('mem')
- parent_weights: float32 [512], P('mem')
All inputs are finite; a program needn't handle non-finite values.
Results may differ from a plain program's by a relative error of at most 0.0003.
Values sent between devices are 32-bit elements; how exact they have to be, the bound alone decides.
No kernel may reach another device: no remote copies, remote signals or barrier semaphores. Data moves between devices by JAX's collectives and lax.ppermute only.
A program may use at most 64 MiB of HBM per device.

v0:
```python
import math
import jax
import jax.numpy as jnp
from jax import lax
from jax.sharding import Mesh
from jax.sharding import PartitionSpec as P

P_SIZE = 512
ITERS = 2
GRP_MEM = ("grp", "mem_0", "mem_1", "mem_2")
MEM = ("mem_0", "mem_1", "mem_2")


def by_axis(value, axes):
    for axis in axes:
        value = lax.psum(value, axis)
    return value


def cut_along(value, dim, size):
    before, after = (value.shape[:dim], value.shape[dim + 1 :])
    return jnp.moveaxis(value.reshape(*before, size, -1, *after), dim, 0)


def summed_on_arrival(value, axis, dim):
    size = lax.axis_size(axis)
    pieces = lax.all_to_all(cut_along(value, dim, size), axis, 0, 0, tiled=True)
    return jnp.sum(pieces, axis=0)


def in_one_piece(arrays, axis, dim, along):
    columns = [a.reshape(*a.shape[:along], -1) for a in arrays]
    both = jnp.concatenate(columns, axis=along)
    filled, at, done = (summed_on_arrival(both, axis, dim), 0, [])
    for a, column in zip(arrays, columns):
        section = filled[..., at : at + column.shape[along]]
        done.append(section.reshape(*section.shape[:along], *a.shape[along:]))
        at += column.shape[along]
    return tuple(done)


def copy_for_each(value, axis):
    size = lax.axis_size(axis)
    return lax.all_to_all(
        jnp.broadcast_to(value[None], (size, *value.shape)), axis, 0, 0, tiled=True
    )


def taken_together(value, axis):
    return copy_for_each(value, axis).sum(axis=0)


def in_one(arrays, axis):
    ends = [0]
    for a in arrays:
        ends.append(ends[-1] + a.size)
    total = taken_together(jnp.concatenate([a.ravel() for a in arrays]), axis)
    return tuple((total[b:e].reshape(a.shape) for a, b, e in zip(arrays, ends, ends[1:])))


def in_one_piece_2(arrays, axis, dim, along):
    columns = [a.reshape(*a.shape[:along], -1) for a in arrays]
    both = jnp.concatenate(columns, axis=along)
    filled, at, done = (lax.all_gather(both, axis, axis=dim, tiled=True), 0, [])
    for a, column in zip(arrays, columns):
        section = filled[..., at : at + column.shape[along]]
        done.append(section.reshape(*section.shape[:along], *a.shape[along:]))
        at += column.shape[along]
    return tuple(done)


def child_features(means, variances):
    return jnp.concatenate([means, variances + means * means], axis=1)


def accumulate(features, extras, weigh):
    row_count = features.shape[0]
    block = math.gcd(row_count, 1024)
    turns = row_count // block
    pieces = (features.reshape(turns, block, features.shape[1]),) + tuple(
        (extra.reshape((turns, block) + extra.shape[1:]) for extra in extras)
    )

    def advance(carry, piece):
        weights = weigh(*piece)
        sums = carry[0] + lax.dot_general(
            weights,
            piece[0],
            (((0,), (0,)), ((), ())),
            precision=lax.Precision.HIGHEST,
            preferred_element_type=jnp.float32,
        )
        counts = carry[1] + jnp.sum(weights, axis=0)
        return ((sums, counts), None)

    start_sums = (
        jnp.zeros((P_SIZE, features.shape[1]), jnp.float32),
        jnp.zeros((P_SIZE,), jnp.float32),
    )
    return lax.scan(advance, start_sums, pieces)[0]


def maximize(counts, sums, total):
    width = sums.shape[1] // 2
    mass = counts + 1.0
    means = sums[:, :width] / mass[:, None]
    second = (sums[:, width:] + 1.0) / mass[:, None]
    return (means, second - means * means, mass / (total + P_SIZE))


def parent_table(means, variances, weights):
    inverse = 1.0 / variances
    table = jnp.concatenate([-2.0 * means * inverse, inverse], axis=1)
    offset = jnp.sum(jnp.log(2.0 * math.pi * variances) + means * means * inverse, axis=1)
    return (table, offset, jnp.log(weights))


def soft_weights(block_features, block_virtual, table, offset, log_weight):
    width = block_features.shape[1] // 2
    cross = lax.dot_general(
        block_features,
        table,
        (((1,), (1,)), ((), ())),
        precision=lax.Precision.HIGHEST,
        preferred_element_type=jnp.float32,
    )
    ell = -0.5 / width * (cross + offset[None, :])
    score = log_weight[None, :] + block_virtual[:, None] * ell
    top = jnp.max(score, axis=1, keepdims=True)
    expd = jnp.exp(score - top)
    resp = expd / jnp.sum(expd, axis=1, keepdims=True)
    return resp * block_virtual[:, None]


def shards(child_means, child_variances, virtual_counts, assignment):
    features = child_features(child_means, child_variances)
    virtual = virtual_counts.astype(jnp.float32)
    labels = jnp.arange(P_SIZE, dtype=jnp.int32)

    def initial_weights(block_features, block_virtual, block_assign):
        return (block_assign == labels[None, :]).astype(jnp.float32) * block_virtual[:, None]

    sums, counts = accumulate(features, (virtual, assignment), initial_weights)
    total = by_axis(jnp.sum(virtual), GRP_MEM)

    def combine(local_sums, local_counts):
        shared = in_one_piece((local_sums, local_counts), MEM, 0, 1)
        return in_one((shared[0], shared[1]), "grp")

    own_sums, own_counts = combine(sums, counts)
    means, variances, weights = maximize(own_counts, own_sums, total)
    for iteration in range(ITERS):
        all_means, all_variances, all_weights = in_one_piece_2(
            (means, variances, weights), MEM, 0, 1
        )
        table, offset, log_weight = parent_table(all_means, all_variances, all_weights)

        def weigh(block_features, block_virtual):
            return soft_weights(block_features, block_virtual, table, offset, log_weight)

        sums, counts = accumulate(features, (virtual,), weigh)
        own_sums, own_counts = combine(sums, counts)
        means, variances, weights = maximize(own_counts, own_sums, total)
    return (means, variances, weights)


def solution(mesh):
    split = Mesh(
        mesh.devices.reshape(mesh.shape["grp"], 4, 4, 2), ("grp", "mem_0", "mem_1", "mem_2")
    )
    return jax.shard_map(
        shards,
        mesh=split,
        in_specs=(P(GRP_MEM, None), P(GRP_MEM, None), P(GRP_MEM), P(GRP_MEM, None)),
        out_specs=(P(MEM, None), P(MEM, None), P(MEM)),
        check_vma=False,
    )
```

profile of v0, /device:TPU:1, one launch (start us, length us, event | category | flops | bytes accessed | tf_op | source)
XLA Modules:
  0.0 213.9 jit_solution(10653394932134514791)
XLA Ops:
  0.6 1.3 multiply_add_fusion.2
  1.9 1.2 pad_maximum_fusion
  3.5 8.4 %while.39 = (s32[]{:T(128)}, f32[512,128]{1,0:T(8,128)S(1)}, f32[512]{0:T(512)S(1)}, s32[2,1024,1]{1,2,0:T(1,128)S(1)}, f32[2,1024]{1,0:T(2,128)S(1)}, /*index=5*/f32[2,1024,128]{2,1,0:T(8,128)S(1)}, s32[]{:T(128)}, s32[]{:T(128)}) while((s32[]{:T(128)}, f32[512,128]{1,0:T(8,128)S(1)}, f32[512]{0:T(512)S(1)}, ...), condition=%wide.region_2.3_spmd.clone, body=%wide.region_0.2_spmd.clone.sunk | while | flops 808059392 | bytes 1089644 | solution.py:100
  3.5 3.8 %fusion.57 = f32[512,128]{1,0:T(8,128)S(1)} fusion(f32[1024]{0:T(1024)S(1)} %bitcast.73, s32[1024]{0:T(1024)S(1)} %bitcast.75, f32[2,1024,128]{2,1,0:T(8,128)S(1)} %get-tuple-element.440, s32[]{:T(128)} %get-tuple-element.427, f32[512,128]{1,0:T(8,128)S(1)} %get-tuple-element.428, pred[]{:T(512)S(6)} %compare.9), kind=kOutput, calls=%fused_computation.5.clone.1 | convolution fusion | flops 806486016 | bytes 1056773 | tf_op jit(solution)/shard_map/while/body/eval_jaxpr/dot_general | solution.py:86
  7.7 3.8 %fusion.57 = f32[512,128]{1,0:T(8,128)S(1)} fusion(f32[1024]{0:T(1024)S(1)} %bitcast.73, s32[1024]{0:T(1024)S(1)} %bitcast.75, f32[2,1024,128]{2,1,0:T(8,128)S(1)} %get-tuple-element.440, s32[]{:T(128)} %get-tuple-element.427, f32[512,128]{1,0:T(8,128)S(1)} %get-tuple-element.428, pred[]{:T(512)S(6)} %compare.9), kind=kOutput, calls=%fused_computation.5.clone.1 | convolution fusion | flops 806486016 | bytes 1056773 | tf_op jit(solution)/shard_map/while/body/eval_jaxpr/dot_general | solution.py:86
  12.1 19.8 %all_to_all.33 = f32[32,16,129]{2,1,0:T(8,128)S(1)} all-to-all(f32[32,16,129]{2,1,0:T(8,128)S(1)} %pad_maximum_fusion.1), channel_id=1, replica_groups=mesh['grp'=8,'mem_0'=4,'mem_1'=4,'mem_2'=2] {'mem_0','mem_1','mem_2'}, dimensions={0} | all-to-all | bytes 528384 | tf_op jit(solution)/shard_map/all_to_all | solution.py:27
  32.1 0.7 broadcast_in_dim.8
  32.8 8.2 %all-to-all-start.1 = ((f32[8,1,2064]{2,1,0:T(1,128)}), f32[8,1,2064]{2,1,0:T(1,128)S(1)}, u32[]{:S(2)}, u32[]{:S(2)}) async-start(f32[8,1,2064]{2,1,0:T(1,128)} %broadcast_in_dim.8), calls=%async_computation.1 | async-start | bytes 139264 | tf_op jit(solution)/shard_map/all_to_all | solution.py:44
  41.6 14.2 %psum.28 = f32[]{:T(128)} all-reduce(f32[]{:T(128)} %convert_reduce_fusion), channel_id=1, replica_groups=mesh['grp'=8,'mem_0'=4,'mem_1'=4,'mem_2'=2] {'grp'}, use_global_device_ids=true, to_apply=%region_6.7 | all-reduce | flops 1 | bytes 8 | tf_op jit(solution)/shard_map/psum | solution.py:16
  55.8 7.2 %psum.29 = f32[]{:T(128)} all-reduce(f32[]{:T(128)} %psum.28), channel_id=1, replica_groups=mesh['grp'=8,'mem_0'=4,'mem_1'=4,'mem_2'=2] {'mem_0'}, use_global_device_ids=true, to_apply=%region_7.8 | all-reduce | flops 1 | bytes 8 | tf_op jit(solution)/shard_map/psum | solution.py:16
  63.0 8.1 %psum.30 = f32[]{:T(128)} all-reduce(f32[]{:T(128)} %psum.29), channel_id=1, replica_groups=mesh['grp'=8,'mem_0'=4,'mem_1'=4,'mem_2'=2] {'mem_1'}, use_global_device_ids=true, to_apply=%region_8.9 | all-reduce | flops 1 | bytes 8 | tf_op jit(solution)/shard_map/psum | solution.py:16
  71.0 10.5 %psum.31 = f32[]{:T(128)} all-reduce(f32[]{:T(128)} %psum.30), channel_id=1, replica_groups=mesh['grp'=8,'mem_0'=4,'mem_1'=4,'mem_2'=2] {'mem_2'}, use_global_device_ids=true, to_apply=%region_9.10 | all-reduce | flops 1 | bytes 8 | tf_op jit(solution)/shard_map/psum | solution.py:16
  82.6 23.0 %all_gather.6 = f32[512,129]{1,0:T(8,128)S(1)} all-gather(f32[16,129]{1,0:T(8,128)S(1)} %pad_maximum_fusion.6), channel_id=1, replica_groups=mesh['grp'=8,'mem_0'=4,'mem_1'=4,'mem_2'=2] {'mem_0','mem_1','mem_2'}, dimensions={0}, use_global_device_ids=true | all-gather | bytes 272448 | tf_op jit(solution)/shard_map/all_gather | solution.py:64
  106.1 12.3 %while.40 = (s32[]{:T(128)}, f32[512,128]{1,0:T(8,128)}, f32[512]{0:T(512)S(1)}, f32[512]{0:T(512)S(1)}, f32[2,1024,128]{2,1,0:T(8,128)S(1)}, /*index=5*/f32[512...) while((s32[]{:T(128)}, f32[512,128]{1,0:T(8,128)}, ...), condition=%wide.region_15.16_spmd.clone, body=%wide.region_11.15_spmd.clone.sunk | while | flops 1617559040 | bytes 10293372 | solution.py:100
  106.1 2.0 fusion.60
  109.0 2.7 %convolution_add_fusion.4 = f32[512,128]{1,0:T(8,128)} fusion(f32[2,1024,128]{2,1,0:T(8,128)S(1)} %get-tuple-element.467, s32[]{:T(128)} %get-tuple-element.453, f32[1024,512]{0,1:T(8,128)S(1)} %get-tuple-element.407, f32[1024]{0:T(1024)S(1)} %bitcast.69, f32[1024]{0:T(1024)S(1)} %fusion.61, f32[1024]{0:T(1024)S(1)} %get-tuple-element.408, ...), kind=kOutput, calls=%fused_computation.20.clone.1 | convolution fusion | flops 807010304 | bytes 3158021 | tf_op jit(solution)/shard_map/while/body/eval_jaxpr/dot_general | solution.py:86
  111.8 2.0 fusion.60
  114.7 3.7 %convolution_add_fusion.4 = f32[512,128]{1,0:T(8,128)} fusion(f32[2,1024,128]{2,1,0:T(8,128)S(1)} %get-tuple-element.467, s32[]{:T(128)} %get-tuple-element.453, f32[1024,512]{0,1:T(8,128)S(1)} %get-tuple-element.407, f32[1024]{0:T(1024)S(1)} %bitcast.69, f32[1024]{0:T(1024)S(1)} %fusion.61, f32[1024]{0:T(1024)S(1)} %get-tuple-element.408, ...), kind=kOutput, calls=%fused_computation.20.clone.1 | convolution fusion | flops 807010304 | bytes 3158021 | tf_op jit(solution)/shard_map/while/body/eval_jaxpr/dot_general | solution.py:86
  118.5 1.0 pad_maximum_fusion.2
  119.5 16.1 %all_to_all.34 = f32[32,16,129]{2,1,0:T(8,128)S(1)} all-to-all(f32[32,16,129]{2,1,0:T(8,128)S(1)} %pad_maximum_fusion.2), channel_id=1, replica_groups=mesh['grp'=8,'mem_0'=4,'mem_1'=4,'mem_2'=2] {'mem_0','mem_1','mem_2'}, dimensions={0} | all-to-all | bytes 528384 | tf_op jit(solution)/shard_map/all_to_all | solution.py:27
  136.5 4.3 %all-to-all-start.3 = ((f32[8,1,2064]{2,1,0:T(1,128)}), f32[8,1,2064]{2,1,0:T(1,128)S(1)}, u32[]{:S(2)}, u32[]{:S(2)}) async-start(f32[8,1,2064]{2,1,0:T(1,128)} %broadcast_in_dim.9), calls=%async_computation.3 | async-start | bytes 139264 | tf_op jit(solution)/shard_map/all_to_all | solution.py:44
  140.7 7.2 %all-to-all-done.3 = f32[8,1,2064]{2,1,0:T(1,128)S(1)} async-done(((f32[8,1,2064]{2,1,0:T(1,128)}), f32[8,1,2064]{2,1,0:T(1,128)S(1)}, u32[]{:S(2)}, u32[]{:S(2)}) %all-to-all-start.3) | async-done | bytes 66080 | tf_op jit(solution)/shard_map/all_to_all | solution.py:44
  148.2 24.9 %all_gather.7 = f32[512,129]{1,0:T(8,128)S(1)} all-gather(f32[16,129]{1,0:T(8,128)S(1)} %pad_maximum_fusion.7), channel_id=1, replica_groups=mesh['grp'=8,'mem_0'=4,'mem_1'=4,'mem_2'=2] {'mem_0','mem_1','mem_2'}, dimensions={0}, use_global_device_ids=true | all-gather | bytes 272448 | tf_op jit(solution)/shard_map/all_gather | solution.py:64
  173.7 12.3 %while.41 = (s32[]{:T(128)}, f32[512,128]{1,0:T(8,128)}, f32[512]{0:T(512)S(1)}, f32[512]{0:T(512)S(1)}, f32[2,1024,128]{2,1,0:T(8,128)S(1)}, /*index=5*/f32[512...) while((s32[]{:T(128)}, f32[512,128]{1,0:T(8,128)}, ...), condition=%wide.region_23.24_spmd.clone, body=%wide.region_19.23_spmd.clone.sunk | while | flops 1617559040 | bytes 10293372 | solution.py:100
  173.8 2.0 fusion.65
  176.7 2.7 %convolution_add_fusion.5 = f32[512,128]{1,0:T(8,128)} fusion(f32[2,1024,128]{2,1,0:T(8,128)S(1)} %get-tuple-element.497, s32[]{:T(128)} %get-tuple-element.483, f32[1024,512]{0,1:T(8,128)S(1)} %get-tuple-element.417, f32[1024]{0:T(1024)S(1)} %bitcast.72, f32[1024]{0:T(1024)S(1)} %fusion.66, f32[1024]{0:T(1024)S(1)} %get-tuple-element.418, ...), kind=kOutput, calls=%fused_computation.35.clone.1 | convolution fusion | flops 807010304 | bytes 3158021 | tf_op jit(solution)/shard_map/while/body/eval_jaxpr/dot_general | solution.py:86
  179.4 2.0 fusion.65
  182.3 3.7 %convolution_add_fusion.5 = f32[512,128]{1,0:T(8,128)} fusion(f32[2,1024,128]{2,1,0:T(8,128)S(1)} %get-tuple-element.497, s32[]{:T(128)} %get-tuple-element.483, f32[1024,512]{0,1:T(8,128)S(1)} %get-tuple-element.417, f32[1024]{0:T(1024)S(1)} %bitcast.72, f32[1024]{0:T(1024)S(1)} %fusion.66, f32[1024]{0:T(1024)S(1)} %get-tuple-element.418, ...), kind=kOutput, calls=%fused_computation.35.clone.1 | convolution fusion | flops 807010304 | bytes 3158021 | tf_op jit(solution)/shard_map/while/body/eval_jaxpr/dot_general | solution.py:86
  186.2 1.0 pad_maximum_fusion.3
  187.2 15.7 %all_to_all.35 = f32[32,16,129]{2,1,0:T(8,128)S(1)} all-to-all(f32[32,16,129]{2,1,0:T(8,128)S(1)} %pad_maximum_fusion.3), channel_id=1, replica_groups=mesh['grp'=8,'mem_0'=4,'mem_1'=4,'mem_2'=2] {'mem_0','mem_1','mem_2'}, dimensions={0} | all-to-all | bytes 528384 | tf_op jit(solution)/shard_map/all_to_all | solution.py:27
  203.1 9.6 %all_to_all.36 = f32[8,1,2064]{2,1,0:T(1,128)S(1)} all-to-all(f32[8,1,2064]{2,1,0:T(1,128)S(1)} %broadcast_in_dim.10), channel_id=1, replica_groups=mesh['grp'=8,'mem_0'=4,'mem_1'=4,'mem_2'=2] {'grp'}, dimensions={0} | all-to-all | bytes 132096 | tf_op jit(solution)/shard_map/all_to_all | solution.py:44
  213.3 0.7 fusion.33
  (82 shorter events, 9.3 us)
Async XLA Ops:
  1.9 1.5 copy-start.1
  1.9 1.5 copy-start
  32.8 49.4 %all-to-all-start.1 = ((f32[8,1,2064]{2,1,0:T(1,128)}), f32[8,1,2064]{2,1,0:T(1,128)S(1)}, u32[]{:S(2)}, u32[]{:S(2)}) async-start(f32[8,1,2064]{2,1,0:T(1,128)} %broadcast_in_dim.8), calls=%async_computation.1 | async-start | bytes 139264 | tf_op jit(solution)/shard_map/all_to_all | solution.py:44
  136.5 11.5 %all-to-all-start.3 = ((f32[8,1,2064]{2,1,0:T(1,128)}), f32[8,1,2064]{2,1,0:T(1,128)S(1)}, u32[]{:S(2)}, u32[]{:S(2)}) async-start(f32[8,1,2064]{2,1,0:T(1,128)} %broadcast_in_dim.9), calls=%async_computation.3 | async-start | bytes 139264 | tf_op jit(solution)/shard_map/all_to_all | solution.py:44
where the time goes:
time: 215 us; the launch traced here: 214 us
  blocking collectives  149 us (69%)
  matrix products  28.5 us (13%)
  starting transfers between devices  12.4 us (6%)
  other arithmetic  11.8 us (5%)
  waiting for transfers between devices  7.2 us (3%)
  local copies, waits for them, and re-layouts  3.24 us (2%)
    all_to_all x3, blocking collectives, summed_on_arrival(): pieces = lax.all_to_all(cut_along(value, dim, size), axis, 0, 0, tiled=True)  51.6 us
    all_gather x2, blocking collectives, in_one_piece_2(): filled, at, done = (lax.all_gather(both, axis, axis=dim, tiled=True), 0, [])  47.9 us
    psum x4, blocking collectives, by_axis(): value = lax.psum(value, axis)  40 us
    dot_general x6, matrix products, advance(): lax.dot_general(weights, piece[0], (((0,), (0,)), ((), ())), precision=la...  20.3 us
    all_to_all x2, starting transfers between devices, copy_for_each(): lax.all_to_all(jnp.broadcast_to(value[None], (size, *value.shape)), axis,...  12.4 us
    all_to_all x1, blocking collectives, copy_for_each(): lax.all_to_all(jnp.broadcast_to(value[None], (size, *value.shape)), axis,...  9.55 us
    dot_general x4, matrix products, soft_weights(): lax.dot_general(block_features, table, (((1,), (1,)), ((), ())), precisio...  8.19 us
    all_to_all x2, waiting for transfers between devices, copy_for_each(): lax.all_to_all(jnp.broadcast_to(value[None], (size, *value.shape)), axis,...  7.2 us
  transfers between devices with their start and end apart: 2, of which 1 were waited for; matrix products, arithmetic and copies ran while one was open for 0% of the time, Pallas kernels for 0%

commit v1 on v0

--- a/solution.py
+++ b/solution.py
@@ -13,7 +13,7 @@
 
 def by_axis(value, axes):
     for axis in axes:
-        value = lax.psum(value, axis)
+        value = jnp.sum(lax.all_gather(value, axis), axis=0)
     return value
 
 

time: 215 us -> 224 us (1.042)
  blocking collectives: 149 us -> 127 us
  waiting for transfers between devices: 7.2 us -> 18.6 us
  starting transfers between devices: 12.4 us -> 21 us
  local copies, waits for them, and re-layouts: 3.24 us -> 11.2 us
  other arithmetic: 11.8 us -> 15 us
    psum x4 -> x0, blocking collectives: 40 us -> none  [by_axis(): value = lax.psum(value, axis)]
    unnamed x0 -> x4, blocking collectives: none -> 37.5 us
    all_to_all x3 -> x2, blocking collectives: 51.6 us -> 31.7 us  [summed_on_arrival(): pieces = lax.all_to_all(cut_along(value, dim, size), axis, 0, 0, tiled=True)]
    all_to_all x0 -> x1, waiting for transfers between devices: none -> 11.4 us  [summed_on_arrival(): pieces = lax.all_to_all(cut_along(value, dim, size), axis, 0, 0, tiled=True)]
    all_to_all x0 -> x1, starting transfers between devices: none -> 8.58 us  [summed_on_arrival(): pieces = lax.all_to_all(cut_along(value, dim, size), axis, 0, 0, tiled=True)]
    unnamed x4 -> x24, local copies, waits for them, and re-layouts: 0.01 us -> 7.98 us
    reduce_sum x0 -> x4, other arithmetic: none -> 2.4 us  [by_axis(): value = jnp.sum(lax.all_gather(value, axis), axis=0)]
  transfers between devices with their start and end apart: 2 -> 3, of which waited for: 1 -> 2; matrix products, arithmetic and copies ran while one was open for 0% -> 5% of each run, Pallas kernels for 0% -> 0%
where the time goes in v1:
time: 224 us; the launch traced here: 223 us
  blocking collectives  127 us (57%)
  matrix products  28.5 us (13%)
  starting transfers between devices  21 us (9%)
  waiting for transfers between devices  18.6 us (8%)
  other arithmetic  15 us (7%)
  local copies, waits for them, and re-layouts  11.2 us (5%)
    all_gather x2, blocking collectives, in_one_piece_2(): filled, at, done = (lax.all_gather(both, axis, axis=dim, tiled=True), 0, [])  47.9 us
    unnamed x4, blocking collectives  37.5 us
    all_to_all x2, blocking collectives, summed_on_arrival(): pieces = lax.all_to_all(cut_along(value, dim, size), axis, 0, 0, tiled=True)  31.7 us
    dot_general x6, matrix products, advance(): lax.dot_general(weights, piece[0], (((0,), (0,)), ((), ())), precision=la...  20.3 us
    all_to_all x2, starting transfers between devices, copy_for_each(): lax.all_to_all(jnp.broadcast_to(value[None], (size, *value.shape)), axis,...  12.4 us
    all_to_all x1, waiting for transfers between devices, summed_on_arrival(): pieces = lax.all_to_all(cut_along(value, dim, size), axis, 0, 0, tiled=True)  11.4 us
    all_to_all x1, blocking collectives, copy_for_each(): lax.all_to_all(jnp.broadcast_to(value[None], (size, *value.shape)), axis,...  9.55 us
    all_to_all x1, starting transfers between devices, summed_on_arrival(): pieces = lax.all_to_all(cut_along(value, dim, size), axis, 0, 0, tiled=True)  8.58 us
  transfers between devices with their start and end apart: 3, of which 2 were waited for; matrix products, arithmetic and copies ran while one was open for 5% of the time, Pallas kernels for 0%

profile of v1, /device:TPU:1, one launch (start us, length us, event | category | flops | bytes accessed | tf_op | source)
XLA Modules:
  0.0 222.8 jit_solution(2434122119322258617)
XLA Ops:
  0.6 1.3 multiply_add_fusion.2
  3.5 8.4 %while.39 = (s32[]{:T(128)}, f32[512,128]{1,0:T(8,128)S(1)}, f32[512]{0:T(512)S(1)}, s32[2,1024,1]{1,2,0:T(1,128)S(1)}, f32[2,1024]{1,0:T(2,128)S(1)}, /*index=5*/f32[2,1024,128]{2,1,0:T(8,128)S(1)}, s32[]{:T(128)}, s32[]{:T(128)}) while((s32[]{:T(128)}, f32[512,128]{1,0:T(8,128)S(1)}, f32[512]{0:T(512)S(1)}, ...), condition=%wide.region_2.3_spmd.clone, body=%wide.region_0.2_spmd.clone.sunk | while | flops 808059392 | bytes 1089644 | solution.py:100
  3.5 3.8 %fusion.57 = f32[512,128]{1,0:T(8,128)S(1)} fusion(f32[1024]{0:T(1024)S(1)} %bitcast.81, s32[1024]{0:T(1024)S(1)} %bitcast.83, f32[2,1024,128]{2,1,0:T(8,128)S(1)} %get-tuple-element.440, s32[]{:T(128)} %get-tuple-element.427, f32[512,128]{1,0:T(8,128)S(1)} %get-tuple-element.428, pred[]{:T(512)S(6)} %compare.9), kind=kOutput, calls=%fused_computation.5.clone.1 | convolution fusion | flops 806486016 | bytes 1056773 | tf_op jit(solution)/shard_map/while/body/eval_jaxpr/dot_general | solution.py:86
  7.7 3.8 %fusion.57 = f32[512,128]{1,0:T(8,128)S(1)} fusion(f32[1024]{0:T(1024)S(1)} %bitcast.81, s32[1024]{0:T(1024)S(1)} %bitcast.83, f32[2,1024,128]{2,1,0:T(8,128)S(1)} %get-tuple-element.440, s32[]{:T(128)} %get-tuple-element.427, f32[512,128]{1,0:T(8,128)S(1)} %get-tuple-element.428, pred[]{:T(512)S(6)} %compare.9), kind=kOutput, calls=%fused_computation.5.clone.1 | convolution fusion | flops 806486016 | bytes 1056773 | tf_op jit(solution)/shard_map/while/body/eval_jaxpr/dot_general | solution.py:86
  13.0 8.6 %all-to-all-start = ((f32[32,16,129]{2,1,0:T(8,128)}), f32[32,16,129]{2,1,0:T(8,128)S(1)}, u32[]{:S(2)}, u32[]{:S(2)}) async-start(f32[32,16,129]{2,1,0:T(8,128)} %pad_maximum_fusion.1), calls=%async_computation | async-start | bytes 1048576 | tf_op jit(solution)/shard_map/all_to_all | solution.py:27
  21.5 11.4 %all-to-all-done = f32[32,16,129]{2,1,0:T(8,128)S(1)} async-done(((f32[32,16,129]{2,1,0:T(8,128)}), f32[32,16,129]{2,1,0:T(8,128)S(1)}, u32[]{:S(2)}, u32[]{:S(2)}) %all-to-all-start) | async-done | bytes 264224 | tf_op jit(solution)/shard_map/all_to_all | solution.py:27
  33.8 8.2 %all-to-all-start.1 = ((f32[8,1,2064]{2,1,0:T(1,128)}), f32[8,1,2064]{2,1,0:T(1,128)S(1)}, u32[]{:S(2)}, u32[]{:S(2)}) async-start(f32[8,1,2064]{2,1,0:T(1,128)} %broadcast_in_dim.8), calls=%async_computation.1 | async-start | bytes 139264 | tf_op jit(solution)/shard_map/all_to_all | solution.py:44
  43.2 1.4 dynamic-update-slice
  44.6 13.4 %all-reduce = f32[8]{0:T(128)S(1)} all-reduce(f32[8]{0:T(128)S(1)} %dynamic-update-slice), channel_id=1, replica_groups=mesh['grp'=8,'mem_0'=4,'mem_1'=4,'mem_2'=2] {'grp'}, use_global_device_ids=true, to_apply=%add | all-reduce | flops 8 | bytes 64
  59.2 1.4 dynamic-update-slice.1
  60.6 6.7 %all-reduce.1 = f32[4]{0:T(128)S(1)} all-reduce(f32[4]{0:T(128)S(1)} %dynamic-update-slice.1), channel_id=1, replica_groups=mesh['grp'=8,'mem_0'=4,'mem_1'=4,'mem_2'=2] {'mem_0'}, use_global_device_ids=true, to_apply=%add.1 | all-reduce | flops 4 | bytes 32
  68.5 1.4 dynamic-update-slice.2
  69.9 7.4 %all-reduce.2 = f32[4]{0:T(128)S(1)} all-reduce(f32[4]{0:T(128)S(1)} %dynamic-update-slice.2), channel_id=1, replica_groups=mesh['grp'=8,'mem_0'=4,'mem_1'=4,'mem_2'=2] {'mem_1'}, use_global_device_ids=true, to_apply=%add.2 | all-reduce | flops 4 | bytes 32
  78.5 1.4 dynamic-update-slice.3
  79.9 9.9 %all-reduce.3 = f32[2]{0:T(128)S(1)} all-reduce(f32[2]{0:T(128)S(1)} %dynamic-update-slice.3), channel_id=1, replica_groups=mesh['grp'=8,'mem_0'=4,'mem_1'=4,'mem_2'=2] {'mem_2'}, use_global_device_ids=true, to_apply=%add.3 | all-reduce | flops 2 | bytes 16
  91.4 23.0 %all_gather.38 = f32[512,129]{1,0:T(8,128)S(1)} all-gather(f32[16,129]{1,0:T(8,128)S(1)} %pad_maximum_fusion.6), channel_id=1, replica_groups=mesh['grp'=8,'mem_0'=4,'mem_1'=4,'mem_2'=2] {'mem_0','mem_1','mem_2'}, dimensions={0}, use_global_device_ids=true | all-gather | bytes 272448 | tf_op jit(solution)/shard_map/all_gather | solution.py:64
  115.0 12.3 %while.40 = (s32[]{:T(128)}, f32[512,128]{1,0:T(8,128)}, f32[512]{0:T(512)S(1)}, f32[512]{0:T(512)S(1)}, f32[2,1024,128]{2,1,0:T(8,128)S(1)}, /*index=5*/f32[512...) while((s32[]{:T(128)}, f32[512,128]{1,0:T(8,128)}, ...), condition=%wide.region_15.16_spmd.clone, body=%wide.region_11.15_spmd.clone.sunk | while | flops 1617559040 | bytes 10293372 | solution.py:100
  115.0 2.0 fusion.60
  117.9 2.7 %convolution_add_fusion.4 = f32[512,128]{1,0:T(8,128)} fusion(f32[2,1024,128]{2,1,0:T(8,128)S(1)} %get-tuple-element.467, s32[]{:T(128)} %get-tuple-element.453, f32[1024,512]{0,1:T(8,128)S(1)} %get-tuple-element.407, f32[1024]{0:T(1024)S(1)} %bitcast.77, f32[1024]{0:T(1024)S(1)} %fusion.61, f32[1024]{0:T(1024)S(1)} %get-tuple-element.408, ...), kind=kOutput, calls=%fused_computation.20.clone.1 | convolution fusion | flops 807010304 | bytes 3158021 | tf_op jit(solution)/shard_map/while/body/eval_jaxpr/dot_general | solution.py:86
  120.6 2.0 fusion.60
  123.5 3.7 %convolution_add_fusion.4 = f32[512,128]{1,0:T(8,128)} fusion(f32[2,1024,128]{2,1,0:T(8,128)S(1)} %get-tuple-element.467, s32[]{:T(128)} %get-tuple-element.453, f32[1024,512]{0,1:T(8,128)S(1)} %get-tuple-element.407, f32[1024]{0:T(1024)S(1)} %bitcast.77, f32[1024]{0:T(1024)S(1)} %fusion.61, f32[1024]{0:T(1024)S(1)} %get-tuple-element.408, ...), kind=kOutput, calls=%fused_computation.20.clone.1 | convolution fusion | flops 807010304 | bytes 3158021 | tf_op jit(solution)/shard_map/while/body/eval_jaxpr/dot_general | solution.py:86
  128.4 16.1 %all_to_all.33 = f32[32,16,129]{2,1,0:T(8,128)S(1)} all-to-all(f32[32,16,129]{2,1,0:T(8,128)S(1)} %pad_maximum_fusion.2), channel_id=1, replica_groups=mesh['grp'=8,'mem_0'=4,'mem_1'=4,'mem_2'=2] {'mem_0','mem_1','mem_2'}, dimensions={0} | all-to-all | bytes 528384 | tf_op jit(solution)/shard_map/all_to_all | solution.py:27
  145.3 4.3 %all-to-all-start.3 = ((f32[8,1,2064]{2,1,0:T(1,128)}), f32[8,1,2064]{2,1,0:T(1,128)S(1)}, u32[]{:S(2)}, u32[]{:S(2)}) async-start(f32[8,1,2064]{2,1,0:T(1,128)} %broadcast_in_dim.9), calls=%async_computation.3 | async-start | bytes 139264 | tf_op jit(solution)/shard_map/all_to_all | solution.py:44
  149.6 7.2 %all-to-all-done.3 = f32[8,1,2064]{2,1,0:T(1,128)S(1)} async-done(((f32[8,1,2064]{2,1,0:T(1,128)}), f32[8,1,2064]{2,1,0:T(1,128)S(1)}, u32[]{:S(2)}, u32[]{:S(2)}) %all-to-all-start.3) | async-done | bytes 66080 | tf_op jit(solution)/shard_map/all_to_all | solution.py:44
  157.1 24.9 %all_gather.39 = f32[512,129]{1,0:T(8,128)S(1)} all-gather(f32[16,129]{1,0:T(8,128)S(1)} %pad_maximum_fusion.7), channel_id=1, replica_groups=mesh['grp'=8,'mem_0'=4,'mem_1'=4,'mem_2'=2] {'mem_0','mem_1','mem_2'}, dimensions={0}, use_global_device_ids=true | all-gather | bytes 272448 | tf_op jit(solution)/shard_map/all_gather | solution.py:64
  182.6 12.3 %while.41 = (s32[]{:T(128)}, f32[512,128]{1,0:T(8,128)}, f32[512]{0:T(512)S(1)}, f32[512]{0:T(512)S(1)}, f32[2,1024,128]{2,1,0:T(8,128)S(1)}, /*index=5*/f32[512...) while((s32[]{:T(128)}, f32[512,128]{1,0:T(8,128)}, ...), condition=%wide.region_23.24_spmd.clone, body=%wide.region_19.23_spmd.clone.sunk | while | flops 1617559040 | bytes 10293372 | solution.py:100
  182.6 2.0 fusion.65
  185.5 2.7 %convolution_add_fusion.5 = f32[512,128]{1,0:T(8,128)} fusion(f32[2,1024,128]{2,1,0:T(8,128)S(1)} %get-tuple-element.497, s32[]{:T(128)} %get-tuple-element.483, f32[1024,512]{0,1:T(8,128)S(1)} %get-tuple-element.417, f32[1024]{0:T(1024)S(1)} %bitcast.80, f32[1024]{0:T(1024)S(1)} %fusion.66, f32[1024]{0:T(1024)S(1)} %get-tuple-element.418, ...), kind=kOutput, calls=%fused_computation.35.clone.1 | convolution fusion | flops 807010304 | bytes 3158021 | tf_op jit(solution)/shard_map/while/body/eval_jaxpr/dot_general | solution.py:86
  188.3 2.0 fusion.65
  191.2 3.7 %convolution_add_fusion.5 = f32[512,128]{1,0:T(8,128)} fusion(f32[2,1024,128]{2,1,0:T(8,128)S(1)} %get-tuple-element.497, s32[]{:T(128)} %get-tuple-element.483, f32[1024,512]{0,1:T(8,128)S(1)} %get-tuple-element.417, f32[1024]{0:T(1024)S(1)} %bitcast.80, f32[1024]{0:T(1024)S(1)} %fusion.66, f32[1024]{0:T(1024)S(1)} %get-tuple-element.418, ...), kind=kOutput, calls=%fused_computation.35.clone.1 | convolution fusion | flops 807010304 | bytes 3158021 | tf_op jit(solution)/shard_map/while/body/eval_jaxpr/dot_general | solution.py:86
  196.1 15.7 %all_to_all.34 = f32[32,16,129]{2,1,0:T(8,128)S(1)} all-to-all(f32[32,16,129]{2,1,0:T(8,128)S(1)} %pad_maximum_fusion.3), channel_id=1, replica_groups=mesh['grp'=8,'mem_0'=4,'mem_1'=4,'mem_2'=2] {'mem_0','mem_1','mem_2'}, dimensions={0} | all-to-all | bytes 528384 | tf_op jit(solution)/shard_map/all_to_all | solution.py:27
  212.0 9.6 %all_to_all.35 = f32[8,1,2064]{2,1,0:T(1,128)S(1)} all-to-all(f32[8,1,2064]{2,1,0:T(1,128)S(1)} %broadcast_in_dim.10), channel_id=1, replica_groups=mesh['grp'=8,'mem_0'=4,'mem_1'=4,'mem_2'=2] {'grp'}, dimensions={0} | all-to-all | bytes 132096 | tf_op jit(solution)/shard_map/all_to_all | solution.py:44
  (107 shorter events, 19.3 us)
Async XLA Ops:
  1.9 1.5 copy-start.1
  1.9 1.5 copy-start
  11.9 30.1 %copy-start.5 = (u32[256]{0:T(256)S(1)}, u32[256]{0:T(256)}, u32[]{:S(2)}) copy-start(u32[256]{0:T(256)} %constant.58) | copy-start | bytes 3076
  11.9 46.1 %copy-start.4 = (u32[256]{0:T(256)S(1)}, u32[256]{0:T(256)}, u32[]{:S(2)}) copy-start(u32[256]{0:T(256)} %constant.63) | copy-start | bytes 3076
  11.9 55.4 %copy-start.3 = (u32[256]{0:T(256)S(1)}, u32[256]{0:T(256)}, u32[]{:S(2)}) copy-start(u32[256]{0:T(256)} %constant.68) | copy-start | bytes 3076
  11.9 65.4 %copy-start.2 = (u32[256]{0:T(256)S(1)}, u32[256]{0:T(256)}, u32[]{:S(2)}) copy-start(u32[256]{0:T(256)} %constant.73) | copy-start | bytes 3076
  13.0 20.0 %all-to-all-start = ((f32[32,16,129]{2,1,0:T(8,128)}), f32[32,16,129]{2,1,0:T(8,128)S(1)}, u32[]{:S(2)}, u32[]{:S(2)}) async-start(f32[32,16,129]{2,1,0:T(8,128)} %pad_maximum_fusion.1), calls=%async_computation | async-start | bytes 1048576 | tf_op jit(solution)/shard_map/all_to_all | solution.py:27
  33.8 57.3 %all-to-all-start.1 = ((f32[8,1,2064]{2,1,0:T(1,128)}), f32[8,1,2064]{2,1,0:T(1,128)S(1)}, u32[]{:S(2)}, u32[]{:S(2)}) async-start(f32[8,1,2064]{2,1,0:T(1,128)} %broadcast_in_dim.8), calls=%async_computation.1 | async-start | bytes 139264 | tf_op jit(solution)/shard_map/all_to_all | solution.py:44
  145.3 11.5 %all-to-all-start.3 = ((f32[8,1,2064]{2,1,0:T(1,128)}), f32[8,1,2064]{2,1,0:T(1,128)S(1)}, u32[]{:S(2)}, u32[]{:S(2)}) async-start(f32[8,1,2064]{2,1,0:T(1,128)} %broadcast_in_dim.9), calls=%async_computation.3 | async-start | bytes 139264 | tf_op jit(solution)/shard_map/all_to_all | solution.py:44
